TPU v7x, 256 devices: a whole 4x4x8 slice. The times are simulated.
256 devices in a mesh: doc: 4 (over x), mem: 64 (over y, z, core).
Axes of the slice: x: 4, y: 4, z: 8, core: 2. Of those that a mesh axis runs over, the one named last changes fastest.
Arguments:
- queries: bfloat16 [65536, 2048], P(('doc', 'mem')), parts along dimension 0, may hold values from -360 to 360, as said below
- grad_out: bfloat16 [65536, 2048], P(('doc', 'mem')), parts along dimension 0, may hold values from -6 to 6
- mem_keys: bfloat16 [1536, 128, 2048], P(('doc', 'mem')), parts along dimension 0, may hold values from -6 to 6
- mem_values: bfloat16 [1536, 128, 2048], P(('doc', 'mem')), parts along dimension 0, may hold values from -6 to 6
- prev_keys: bfloat16 [512, 128, 2048], P(('doc', 'mem')), parts along dimension 0, may hold values from -6 to 6
- prev_values: bfloat16 [512, 128, 2048], P(('doc', 'mem')), parts along dimension 0, may hold values from -6 to 6
- gate_logit: float32 [16], replicated, may hold values from -2 to 2
- location: int32 [1536], P('doc'), parts along dimension 0, may hold values from 0 to 383, as said below
- top_blocks: int32 [512, 16, 4], P(('doc', 'mem')), parts along dimension 0, may hold values from 0 to 383, as said below
- write_slot: int32 [512], P(('doc', 'mem')), parts along dimension 0, may hold values from 0 to 5, as said below
Outputs:
- attended: bfloat16 [65536, 2048], P(('doc', 'mem')), parts along dimension 0
- query_grad: bfloat16 [65536, 2048], P(('doc', 'mem')), parts along dimension 0
- gate_grad: float32 [64], P('doc'), parts along dimension 0
There are 4 independent parts, one for each index of `doc`. A program takes and returns all parts, laid end to end along the dimension named above; an argument that names none is the same for every part. Nothing has to cross between parts.
Inputs may be any that keep to these rules, and one draw needn't show every extreme that they name: `queries`: values of a row between 6 and 360 in magnitude only through a common row factor. A permutation: memory block j lies in storage slot location[j], which belongs to shard location[j] // 6. `top_blocks`: the 4 blocks of one (b, h) are distinct. Over the rows of one shard, at most 4 entries name blocks whose slots belong to any one shard, and these form at most 2 distinct (block, head) pairs; for each shard both bounds are reached at some shard. `write_slot`: distinct within each aligned group of 2 entries.
All inputs are finite; a program needn't handle non-finite values.
Results may differ from a plain program's by a relative error of at most 0.005.
Values may be sent and summed in bfloat16 or wider, within the bound.
A program may use at most 128 MiB of HBM per device.

v0:
```python
import jax
import jax.numpy as jnp
from jax import lax
from jax.sharding import PartitionSpec as P


def sent_together(arrays, axis, split_dim, concat_dim, along):
    both = jnp.concatenate(arrays, axis=along)
    filled, at, finished = (
        lax.all_to_all(both, axis, split_axis=split_dim, concat_axis=concat_dim, tiled=True),
        0,
        [],
    )
    for a in arrays:
        finished.append(lax.slice_in_dim(filled, at, at + a.shape[along], axis=along))
        at += a.shape[along]
    return tuple(finished)


def from_behind(block, axis, distance):
    devices = range(lax.axis_size(axis))
    route = [(i - distance, i) for i in devices if i - distance in devices]
    return lax.ppermute(block, axis, route)


def copy_for_each(x, axis):
    length = lax.axis_size(axis)
    return lax.all_to_all(jnp.broadcast_to(x[None], (length, *x.shape)), axis, 0, 0, tiled=True)


def taken_together(x, axis):
    return copy_for_each(x, axis).sum(axis=0)


def head_major(blocks, head_count):
    block_count, row_count, row_width = blocks.shape
    return blocks.reshape(block_count, row_count, head_count, row_width // head_count).transpose(
        0, 2, 1, 3
    )


def token_major(blocks):
    block_count, head_count, row_count, head_dim = blocks.shape
    return blocks.transpose(0, 2, 1, 3).reshape(block_count * row_count, head_count * head_dim)


def attend_blocks(query_rows, grad_rows, key_rows, value_rows, share_of, offset, score_scale):
    raw_scores = jnp.einsum(
        "nhqd,nhkd->nhqk", query_rows, key_rows, preferred_element_type=jnp.float32
    )
    if offset is None:
        scores = raw_scores * score_scale
    else:
        scores = raw_scores * score_scale + offset[:, None, None, :]
    highest = jnp.max(scores, axis=-1, keepdims=True)
    expanded = jnp.exp(scores - highest)
    weights = expanded / jnp.sum(expanded, axis=-1, keepdims=True)
    result = jnp.einsum(
        "nhqk,nhkd->nhqd",
        weights.astype(jnp.bfloat16),
        value_rows,
        preferred_element_type=jnp.float32,
    )
    weight_grad = jnp.einsum(
        "nhqd,nhkd->nhqk", grad_rows, value_rows, preferred_element_type=jnp.float32
    )
    inner = jnp.sum(weights * weight_grad, axis=-1, keepdims=True)
    score_grad = (weights * (weight_grad - inner) * share_of[None, :, None, None]).astype(
        jnp.bfloat16
    )
    query_grad = jnp.einsum(
        "nhqk,nhkd->nhqd", score_grad, key_rows, preferred_element_type=jnp.float32
    )
    return (result, query_grad)


def route_table(top_blocks, location, stored):
    query_count, head_count, pick_count = top_blocks.shape
    item_count = query_count * head_count * pick_count
    slot_ids = jnp.take(location, top_blocks.reshape(item_count), axis=0)
    owner_ids = slot_ids // stored
    item_ids = jnp.arange(item_count, dtype=jnp.int32)
    head_ids = item_ids // pick_count % head_count
    code_ids = slot_ids % stored * head_count + head_ids
    earlier = item_ids[None, :] < item_ids[:, None]
    same_owner = owner_ids[:, None] == owner_ids[None, :]
    pair_ids = slot_ids * head_count + head_ids
    same_pair = pair_ids[:, None] == pair_ids[None, :]
    leading = jnp.logical_not(jnp.any(same_pair & earlier, axis=1))
    lead_rank = jnp.sum(same_owner & earlier & leading[None, :], axis=1)
    position = jnp.sum(jnp.where(same_pair & leading[None, :], lead_rank[None, :], 0), axis=1)
    return (owner_ids, position, code_ids, leading)


def local(
    queries,
    grad_out,
    mem_keys,
    mem_values,
    prev_keys,
    prev_values,
    gate_logit,
    location,
    top_blocks,
    write_slot,
):
    mem_count = lax.axis_size("mem")
    query_count, head_count, pick_count = top_blocks.shape
    stored, block_rows, row_width = mem_keys.shape
    head_dim = row_width // head_count
    score_scale = head_dim ** (-0.5)
    unique_count = head_count * (pick_count // 2) * (query_count + 1)
    distinct_cap = (unique_count + mem_count - 1) // mem_count
    owner_ids, position, code_ids, is_live = route_table(top_blocks, location, stored)
    target = jnp.where(is_live, owner_ids * distinct_cap + position, mem_count * distinct_cap)
    outgoing = (
        jnp.full((mem_count * distinct_cap,), -1, jnp.int32).at[target].set(code_ids, mode="drop")
    )
    incoming = lax.all_to_all(
        outgoing.reshape(mem_count, distinct_cap), "mem", split_axis=0, concat_axis=0, tiled=True
    )
    key_table = (
        head_major(mem_keys, head_count).at[write_slot].set(head_major(prev_keys, head_count))
    )
    value_table = (
        head_major(mem_values, head_count).at[write_slot].set(head_major(prev_values, head_count))
    )
    key_table = key_table.reshape(stored * head_count, block_rows, head_dim)
    value_table = value_table.reshape(stored * head_count, block_rows, head_dim)
    wanted = jnp.maximum(incoming, 0).reshape(mem_count * distinct_cap)
    served_keys = jnp.take(key_table, wanted, axis=0).reshape(
        mem_count, distinct_cap, block_rows, head_dim
    )
    served_values = jnp.take(value_table, wanted, axis=0).reshape(
        mem_count, distinct_cap, block_rows, head_dim
    )
    fetched_keys, fetched_values = sent_together((served_keys, served_values), "mem", 0, 0, 1)
    memory_keys = fetched_keys[owner_ids, position].reshape(
        query_count, head_count, pick_count * block_rows, head_dim
    )
    memory_values = fetched_values[owner_ids, position].reshape(
        query_count, head_count, pick_count * block_rows, head_dim
    )
    carried = from_behind((prev_keys[-1:], prev_values[-1:]), "mem", 1)
    older_keys = jnp.concatenate([carried[0], prev_keys[:-1]], axis=0)
    older_values = jnp.concatenate([carried[1], prev_values[:-1]], axis=0)
    local_keys = jnp.concatenate(
        [head_major(older_keys, head_count), head_major(prev_keys, head_count)], axis=2
    )
    local_values = jnp.concatenate(
        [head_major(older_values, head_count), head_major(prev_values, head_count)], axis=2
    )
    block_ids = lax.axis_index("mem") * query_count + jnp.arange(query_count, dtype=jnp.int32)
    column_ids = jnp.arange(2 * block_rows, dtype=jnp.int32)
    local_allowed = (block_ids[:, None] > 0) | (column_ids[None, :] >= block_rows)
    local_offset = jnp.where(local_allowed, 0.0, -jnp.inf).astype(jnp.float32)
    query_heads = head_major(queries.reshape(query_count, block_rows, row_width), head_count)
    grad_heads = head_major(grad_out.reshape(query_count, block_rows, row_width), head_count)
    mixing = jax.nn.sigmoid(gate_logit)
    memory_result, memory_grad = attend_blocks(
        query_heads, grad_heads, memory_keys, memory_values, mixing, None, score_scale
    )
    local_result, local_grad = attend_blocks(
        query_heads, grad_heads, local_keys, local_values, 1.0 - mixing, local_offset, score_scale
    )
    blend_of = mixing[None, :, None, None]
    attended = token_major(blend_of * memory_result + (1.0 - blend_of) * local_result).astype(
        jnp.bfloat16
    )
    query_grad = token_major((memory_grad + local_grad) * score_scale).astype(jnp.bfloat16)
    gate_term = (
        jnp.sum(grad_heads.astype(jnp.float32) * (memory_result - local_result), axis=(0, 2, 3))
        * mixing
        * (1.0 - mixing)
    )
    gate_grad = taken_together(gate_term, "mem")
    return (attended, query_grad, gate_grad)


def solution(mesh):
    in_specs = (
        P(("doc", "mem"), None),
        P(("doc", "mem"), None),
        P(("doc", "mem"), None, None),
        P(("doc", "mem"), None, None),
        P(("doc", "mem"), None, None),
        P(("doc", "mem"), None, None),
        P(),
        P("doc"),
        P(("doc", "mem"), None, None),
        P(("doc", "mem")),
    )
    out_specs = (P(("doc", "mem"), None), P(("doc", "mem"), None), P("doc"))
    return jax.shard_map(local, mesh=mesh, in_specs=in_specs, out_specs=out_specs, check_vma=False)
```

profile of v0, /device:TPU:6, one launch (start us, length us, event | category | flops | bytes accessed | tf_op | source)
XLA Modules:
  0.0 381.9 jit_solution(10579187755659775972)
XLA Ops:
  0.6 0.0 copy-start
  0.6 0.8 copy.94
  1.4 0.1 reshape.377
  1.5 0.1 reshape.376
  1.7 1.3 gather_fusion
  3.0 0.2 fusion.52
  3.2 0.2 convert_reduce_fusion
  3.4 0.2 select_reduce_fusion
  3.6 1.0 scatter_custom_fusion.1
  4.6 0.7 all_to_all.13
  5.3 12.1 %all-to-all-start = ((s32[64,1,2]{2,1,0:T(1,128)}), s32[64,1,2]{2,1,0:T(1,128)S(1)}, u32[]{:S(2)}, u32[]{:S(2)}) async-start(s32[64,1,2]{2,1,0:T(1,128)} %bitcast.5), calls=%async_computation | async-start | bytes 65536 | tf_op jit(solution)/shard_map/all_to_all | solution.py:119
  17.4 1.6 copy.99
  19.1 0.7 compare_select_fusion.6
  19.7 1.3 copy.100
  21.1 4.7 %copy.97 = bf16[6,128,2048]{1,2,0:T(8,128)(2,1)} copy(bf16[6,128,2048]{2,1,0:T(8,128)(2,1)} %param.14) | data formatting | bytes 6291456 | tf_op args[2]
  25.7 3.5 copy.98
  29.3 2.3 copy.103
  31.5 2.3 copy.104
  33.8 4.7 %copy.101 = bf16[6,128,2048]{1,2,0:T(8,128)(2,1)} copy(bf16[6,128,2048]{2,1,0:T(8,128)(2,1)} %param.15) | data formatting | bytes 6291456 | tf_op args[3]
  38.5 4.7 %copy.102 = bf16[6,128,16,128]{3,1,2,0:T(8,128)(2,1)} copy(bf16[6,128,16,128]{1,3,2,0:T(8,128)(2,1)} %bitcast.160) | data formatting | bytes 6291456 | tf_op jit(solution)/shard_map/reshape | solution.py:37
  43.2 1.9 scatter_fusion
  45.1 3.2 scatter_fusion.1
  48.3 0.1 maximum_reduce_fusion
  48.4 0.1 max.9
  48.6 3.1 gather_fusion.3
  51.6 4.9 %gather_fusion.4 = bf16[128,128,128]{2,1,0:T(8,128)(2,1)} fusion(bf16[96,128,128]{2,1,0:T(8,128)(2,1)} %bitcast.152, s32[1024]{0:T(1024)S(1)} %pad_clamp_fusion), kind=kCustom, calls=%fused_computation.1.clone | custom fusion | bytes 8389120 | tf_op jit(solution)/shard_map/jit(_take)/gather | solution.py:134
  56.5 5.9 %broadcast_select_fusion.1 = (bf16[128,128,128]{2,1,0:T(8,128)(2,1)}, bf16[128,128,128]{2,1,0:T(8,128)(2,1)}) fusion(bf16[128,128,128]{2,1,0:T(8,128)(2,1)} %gather_fusion.3, pred[128]{0:T(512)(128)(4,1)S(1)} %compare_and_fusion.2, bf16[128,128,128]{2,1,0:T(8,128)(2,1)} %gather_fusion.4), kind=kLoop, calls=%fused_computation.40 | loop fusion | flops 4194304 | bytes 16777344 | tf_op jit(solution)/shard_map/jit(_take)/select_n | solution.py:131
  62.5 7.4 %pad_maximum_fusion = bf16[64,4,128,128]{3,2,1,0:T(8,128)(2,1)} fusion(bf16[64,2,128,128]{3,2,1,0:T(8,128)(2,1)} %bitcast.158, bf16[64,2,128,128]{3,2,1,0:T(8,128)(2,1)} %bitcast.157), kind=kLoop, calls=%fused_computation.12 | loop fusion | flops 4194304 | bytes 16777216 | tf_op jit(solution)/shard_map/concatenate | solution.py:8
  69.9 10.6 %all-to-all-start.1 = ((bf16[64,4,128,128]{3,2,1,0:T(8,128)(2,1)}), bf16[64,4,128,128]{3,2,1,0:T(8,128)(2,1)}, u32[]{:S(2)}, u32[]{:S(2)}) async-start(bf16[64,4,128,128]{3,2,1,0:T(8,128)(2,1)} %pad_maximum_fusion), calls=%async_computation.1 | async-start | bytes 16777216 | tf_op jit(solution)/shard_map/all_to_all | solution.py:10
  80.5 1.1 fusion.80
  81.6 2.7 collective-permute-start
  84.3 1.1 fusion.81
  85.4 3.5 collective-permute-start.1
  88.9 1.5 copy.125
  90.4 1.5 copy.127
  91.9 0.1 or_select_fusion
  92.0 2.2 pad_maximum_fusion.7
  94.2 2.3 copy.109
  96.5 2.3 pad_maximum_fusion.8
  98.7 2.3 copy.112
  101.0 2.1 fusion.39
  103.1 2.7 fusion.38
  105.8 1.4 fusion.82
  107.3 1.9 copy-done.8
  109.2 2.1 fusion.28
  111.3 154.0 %all-to-all-done.1 = bf16[64,4,128,128]{3,2,1,0:T(8,128)(2,1)} async-done(((bf16[64,4,128,128]{3,2,1,0:T(8,128)(2,1)}), bf16[64,4,128,128]{3,2,1,0:T(8,128)(2,1)}, u32[]{:S(2)}, u32[]{:S(2)}) %all-to-all-start.1) | async-done | bytes 8388640 | tf_op jit(solution)/shard_map/all_to_all | solution.py:10
  265.3 6.0 %fusion.79 = (bf16[64,2,128,128]{3,2,1,0:T(8,128)(2,1)}, bf16[64,2,128,128]{3,2,1,0:T(8,128)(2,1)}) fusion(bf16[64,4,128,128]{3,2,1,0:T(8,128)(2,1)} %all-to-all-done.1), kind=kLoop, calls=%fused_computation.134 | loop fusion | bytes 16777216 | tf_op jit(solution)/shard_map/slice | solution.py:15
  271.3 5.4 %gather_fusion.1 = bf16[128,128,128]{2,1,0:T(8,128)(2,1)} fusion(bf16[64,2,128,128]{3,2,1,0:T(8,128)(2,1)} %get-tuple-element.10, s32[128]{0:T(128)S(1)} %get-tuple-element.6), kind=kCustom, calls=%fused_computation.3 | custom fusion | bytes 8389632 | tf_op jit(solution)/shard_map/gather | solution.py:138
  276.7 3.4 fusion.45
  280.1 4.8 %fusion.83 = (f32[2,16,128]{2,1,0:T(8,128)S(1)}, f32[2,16,128,512]{2,3,1,0:T(8,128)}) fusion(f32[2,16,512,128]{3,2,1,0:T(8,128)S(1)} %fusion.45), kind=kOutput, calls=%fused_computation.138 | output fusion | flops 8389119 | bytes 16793600 | tf_op jit(solution)/shard_map/sub | solution.py:56
  284.9 1.0 copy-done.2
  286.0 5.3 %gather_fusion.2 = bf16[128,128,128]{2,1,0:T(8,128)(2,1)} fusion(bf16[64,2,128,128]{3,2,1,0:T(8,128)(2,1)} %get-tuple-element.11, s32[128]{0:T(128)S(1)} %get-tuple-element.6), kind=kCustom, calls=%fused_computation.4 | custom fusion | bytes 8389632 | tf_op jit(solution)/shard_map/gather | solution.py:141
  291.2 6.7 %fusion.42 = f32[2,16,512,128]{3,2,1,0:T(8,128)} fusion(bf16[2,16,512,128]{3,2,1,0:T(8,128)(2,1)} %bitcast.155, bf16[2,128,16,128]{3,2,1,0:T(8,128)(2,1)S(1)} %bitcast.170), kind=kOutput, calls=%fused_computation.64 | convolution fusion | flops 536870912 | bytes 13631488 | tf_op jit(solution)/shard_map/nhqd,nhkd->nhqk/dot_general | solution.py:64
  297.9 12.8 %multiply_reduce_fusion = (f32[16]{0:T(128)S(1)}, f32[2,16,128,128]{3,2,1,0:T(8,128)}) fusion(f32[2,16,128,128]{3,2,1,0:T(8,128)} %fusion.28, bf16[2,128,16,128]{3,2,1,0:T(8,128)(2,1)S(1)} %bitcast.171, bf16[2,16,512,128]{3,2,1,0:T(8,128)(2,1)} %bitcast.156, f32[2,16,128]{2,1,0:T(8,128)S(1)} %get-tuple-element.22, f32[2,16,512,128]{3,2,1,0:T(8,128)} %copy-done.2), kind=kOutput, calls=%fused_computation.45 | convolution fusion | flops 549458432 | bytes 17842240 | tf_op jit(solution)/shard_map/nhqk,nhkd->nhqd/dot_general | solution.py:58
  310.8 2.8 fusion.40
  313.6 0.7 copy.114
  314.3 9.1 %fusion.26 = f32[2,16,128,128]{3,2,1,0:T(8,128)} fusion(f32[2,16,256,128]{3,2,1,0:T(8,128)} %fusion.38, f32[16]{0:T(128)S(1)} %broadcast_subtract_fusion, bf16[2,16,128,128]{3,2,1,0:T(8,128)(2,1)S(1)} %bitcast.163, bf16[2,16,128,128]{3,2,1,0:T(8,128)(2,1)S(1)} %bitcast.175, f32[2,16,128,256]{2,3,1,0:T(8,128)} %copy-done.8, ...), kind=kOutput, calls=%fused_computation.42 | convolution fusion | flops 279974144 | bytes 12599360 | tf_op jit(solution)/shard_map/nhqk,nhkd->nhqd/dot_general | solution.py:71
  323.4 14.4 %fusion.35 = bf16[2,128,16,128]{3,1,2,0:T(8,128)(2,1)S(1)} fusion(f32[2,16,128,128]{3,2,1,0:T(8,128)} %fusion.26, bf16[2,16,512,128]{3,2,1,0:T(8,128)(2,1)} %bitcast.154, f32[2,16,512,128]{3,2,1,0:T(8,128)} %fusion.42, f32[16]{0:T(128)S(1)} %get-tuple-element.5, f32[2,16,128,512]{2,3,1,0:T(8,128)} %get-tuple-element.23, f32[2,16,128]{2,1,0:T(8,128)S(1)} %get-tuple-element.22), kind=kOutput, calls=%fused_computation.55 | convolution fusion | flops 553128448 | bytes 24133696 | tf_op jit(solution)/shard_map/nhqk,nhkd->nhqd/dot_general | solution.py:71
  337.8 0.7 copy.118
  338.5 0.6 broadcast_in_dim.56
  339.1 32.6 %all-to-all-start.2 = ((f32[64,1,16]{2,1,0:T(1,128)}), f32[64,1,16]{2,1,0:T(1,128)S(1)}, u32[]{:S(2)}, u32[]{:S(2)}) async-start(f32[64,1,16]{2,1,0:T(1,128)} %broadcast_in_dim.56), calls=%async_computation.2 | async-start | bytes 65536 | tf_op jit(solution)/shard_map/all_to_all | solution.py:28
  371.7 1.8 copy_bitcast_fusion
  373.6 7.7 %all-to-all-done.2 = f32[64,1,16]{2,1,0:T(1,128)S(1)} async-done(((f32[64,1,16]{2,1,0:T(1,128)}), f32[64,1,16]{2,1,0:T(1,128)S(1)}, u32[]{:S(2)}, u32[]{:S(2)}) %all-to-all-start.2) | async-done | bytes 4128 | tf_op jit(solution)/shard_map/all_to_all | solution.py:28
  381.3 0.6 reduce_sum.82
  (40 shorter events, 0.2 us)
Async XLA Ops:
  0.6 1.0 copy-start
  5.3 43.0 %all-to-all-start = ((s32[64,1,2]{2,1,0:T(1,128)}), s32[64,1,2]{2,1,0:T(1,128)S(1)}, u32[]{:S(2)}, u32[]{:S(2)}) async-start(s32[64,1,2]{2,1,0:T(1,128)} %bitcast.5), calls=%async_computation | async-start | bytes 65536 | tf_op jit(solution)/shard_map/all_to_all | solution.py:119
  19.1 6.7 %copy-start.6 = (bf16[2,128,2048]{1,2,0:T(8,128)(2,1)}, bf16[2,128,2048]{1,2,0:T(8,128)(2,1)S(1)}, u32[]{:S(2)}) copy-start(bf16[2,128,2048]{1,2,0:T(8,128)(2,1)S(1)} %copy.99) | copy-start | bytes 3145732
  69.9 10.7 %copy-start.7 = (bf16[2,128,2048]{1,2,0:T(8,128)(2,1)S(1)}, bf16[2,128,2048]{1,2,0:T(8,128)(2,1)}, u32[]{:S(2)}) copy-start(bf16[2,128,2048]{1,2,0:T(8,128)(2,1)} %copy-done.6) | copy-start | bytes 3145732
  69.9 14.4 %copy-start.5 = (bf16[2,128,2048]{1,2,0:T(8,128)(2,1)S(1)}, bf16[2,128,2048]{1,2,0:T(8,128)(2,1)}, u32[]{:S(2)}) copy-start(bf16[2,128,2048]{1,2,0:T(8,128)(2,1)} %copy.103) | copy-start | bytes 3145732
  69.9 195.4 %all-to-all-start.1 = ((bf16[64,4,128,128]{3,2,1,0:T(8,128)(2,1)}), bf16[64,4,128,128]{3,2,1,0:T(8,128)(2,1)}, u32[]{:S(2)}, u32[]{:S(2)}) async-start(bf16[64,4,128,128]{3,2,1,0:T(8,128)(2,1)} %pad_maximum_fusion), calls=%async_computation.1 | async-start | bytes 16777216 | tf_op jit(solution)/shard_map/all_to_all | solution.py:10
  81.6 10.4 %collective-permute-start = (bf16[1,128,2048]{1,2,0:T(8,128)(2,1)}, bf16[1,128,2048]{1,2,0:T(8,128)(2,1)}, u32[]{:S(2)}, u32[]{:S(2)}) collective-permute-start(bf16[1,128,2048]{1,2,0:T(8,128)(2,1)} %get-tuple-element.12), channel_id=1, source_target_pairs={{0,1},{1,2},{2,3},{3,4},{4,5},{5,6},{6,7},{7,8},{8,9},{9,10},{10,1... | collective-permute-start | bytes 1572872 | tf_op jit(solution)/shard_map/ppermute | solution.py:23
  85.4 11.1 %collective-permute-start.1 = (bf16[1,128,2048]{1,2,0:T(8,128)(2,1)}, bf16[1,128,2048]{1,2,0:T(8,128)(2,1)}, u32[]{:S(2)}, u32[]{:S(2)}) collective-permute-start(bf16[1,128,2048]{1,2,0:T(8,128)(2,1)} %get-tuple-element.14), channel_id=1, source_target_pairs={{0,1},{1,2},{2,3},{3,4},{4,5},{5,6},{6,7},{7,8},{8,9},{9,10},{10,1... | collective-permute-start | bytes 1572872 | tf_op jit(solution)/shard_map/ppermute | solution.py:23
  88.9 3.1 copy-start.11
  92.0 9.0 %copy-start.3 = (bf16[2,128,16,128]{3,1,2,0:T(8,128)(2,1)S(1)}, bf16[2,128,16,128]{3,1,2,0:T(8,128)(2,1)}, u32[]{:S(2)}) copy-start(bf16[2,128,16,128]{3,1,2,0:T(8,128)(2,1)} %copy.100) | copy-start | bytes 3145732
  101.0 2.1 copy-start.4
  101.0 2.1 copy-start.10
  107.3 1.9 copy-start.8
  280.1 5.8 %copy-start.2 = (f32[2,16,512,128]{3,2,1,0:T(8,128)}, f32[2,16,512,128]{3,2,1,0:T(8,128)S(1)}, u32[]{:S(2)}) copy-start(f32[2,16,512,128]{3,2,1,0:T(8,128)S(1)} %fusion.45) | copy-start | bytes 25165828
  297.9 12.8 %copy-start.12 = (f32[16]{0:T(128)S(1)}, f32[16]{0:T(128)}, u32[]{:S(2)}) copy-start(f32[16]{0:T(128)} %param.18) | copy-start | bytes 196
  310.7 3.6 copy-start.9
  323.4 58.4 %copy-start.1 = (s32[384]{0:T(512)S(1)}, s32[384]{0:T(512)}, u32[]{:S(2)}) copy-start(s32[384]{0:T(512)} %param.19) | copy-start | bytes 4612
  339.1 42.2 %all-to-all-start.2 = ((f32[64,1,16]{2,1,0:T(1,128)}), f32[64,1,16]{2,1,0:T(1,128)S(1)}, u32[]{:S(2)}, u32[]{:S(2)}) async-start(f32[64,1,16]{2,1,0:T(1,128)} %broadcast_in_dim.56), calls=%async_computation.2 | async-start | bytes 65536 | tf_op jit(solution)/shard_map/all_to_all | solution.py:28
where the time goes:
time: 384 us; the launch traced here: 382 us
  waiting for transfers between devices  162 us (42%)
  local copies, waits for them, and re-layouts  75.4 us (20%)
  starting transfers between devices  61.6 us (16%)
  matrix products  53.3 us (14%)
  other arithmetic  29 us (8%)
    all_to_all x1, waiting for transfers between devices, sent_together(): lax.all_to_all(both, axis, split_axis=split_dim, concat_axis=concat_dim,...  154 us
    all_to_all x1, starting transfers between devices, copy_for_each(): lax.all_to_all(jnp.broadcast_to(x[None], (length, *x.shape)), axis, 0, 0,...  32.6 us
    dot_general x2, matrix products, attend_blocks(): jnp.einsum('nhqk,nhkd->nhqd', score_grad, key_rows, preferred_element_typ...  23.5 us
    unnamed x33, local copies, waits for them, and re-layouts  20 us
    reshape x6, local copies, waits for them, and re-layouts, head_major(): blocks.reshape(block_count, row_count, head_count, row_width // head_count)  16.3 us
    dot_general x2, matrix products, attend_blocks(): jnp.einsum('nhqk,nhkd->nhqd', weights.astype(jnp.bfloat16), value_rows, p...  14.9 us
    all_to_all x1, starting transfers between devices, local(): lax.all_to_all(outgoing.reshape(mem_count, distinct_cap), 'mem', split_ax...  12.1 us
    all_to_all x1, starting transfers between devices, sent_together(): lax.all_to_all(both, axis, split_axis=split_dim, concat_axis=concat_dim,...  10.6 us
  transfers between devices with their start and end apart: 5, of which 2 were waited for; matrix products, arithmetic and copies ran while one was open for 14% of the time, Pallas kernels for 0%

commit v1 on v0

v1 whole, which is shorter than its diff:
```python
import functools

import jax
import jax.numpy as jnp
from jax import lax
from jax.experimental import pallas as pl
from jax.experimental.pallas import tpu as pltpu
from jax.sharding import PartitionSpec as P

MESH = pl.DeviceIdType.MESH
Z_CHIPS = 8
CORES = 2
LOG2_E = 1.4426950408889634


def route_table(top_blocks, location, stored):
    query_count, head_count, pick_count = top_blocks.shape
    item_count = query_count * head_count * pick_count
    slot_ids = jnp.take(location, top_blocks.reshape(item_count), axis=0)
    owner_ids = slot_ids // stored
    item_ids = jnp.arange(item_count, dtype=jnp.int32)
    head_ids = item_ids // pick_count % head_count
    code_ids = head_ids * stored + slot_ids % stored
    earlier = item_ids[None, :] < item_ids[:, None]
    same_owner = owner_ids[:, None] == owner_ids[None, :]
    pair_ids = slot_ids * head_count + head_ids
    same_pair = pair_ids[:, None] == pair_ids[None, :]
    leading = jnp.logical_not(jnp.any(same_pair & earlier, axis=1))
    lead_rank = jnp.sum(same_owner & earlier & leading[None, :], axis=1)
    position = jnp.sum(jnp.where(same_pair & leading[None, :], lead_rank[None, :], 0), axis=1)
    return (owner_ids, position, code_ids, leading)


def peer_of(step, me, mem_count):
    y_chips = mem_count // (Z_CHIPS * CORES)
    y, z, c = me // (Z_CHIPS * CORES), lax.rem(me // CORES, Z_CHIPS), lax.rem(me, CORES)
    turn = step // Z_CHIPS
    place = lax.rem(step + Z_CHIPS - 1, Z_CHIPS)
    dz = Z_CHIPS // 2 + ((place + 1) // 2) * (1 - 2 * lax.rem(place, 2))
    dy = lax.rem(turn // CORES + 2 * y_chips - dz, y_chips)
    dc = lax.rem(turn, CORES)
    return (lax.rem(y + dy, y_chips) * Z_CHIPS + lax.rem(z + dz, Z_CHIPS)) * CORES + lax.rem(
        c + dc, CORES
    )


def across(a, b):
    return lax.dot_general(a, b, (((1,), (1,)), ((), ())), preferred_element_type=jnp.float32)


def onto(a, b):
    return lax.dot_general(a, b, (((1,), (0,)), ((), ())), preferred_element_type=jnp.float32)


def softmax(raw, scale):
    highest = jnp.max(raw, axis=-1, keepdims=True)
    expanded = jnp.exp2((raw - highest) * (scale * LOG2_E))
    return expanded * (1.0 / jnp.sum(expanded, axis=-1, keepdims=True))


def kernel(
    mem_count,
    head_count,
    pick_count,
    q_hbm,
    g_hbm,
    mk_hbm,
    mv_hbm,
    pk_hbm,
    pv_hbm,
    codes_ref,
    where_ref,
    place_ref,
    gate_ref,
    att_ref,
    qg_ref,
    gate_out_ref,
    q_buf,
    g_buf,
    k_table,
    v_table,
    halo,
    k_send,
    v_send,
    k_got,
    v_got,
    code_got,
    code_smem,
    local_out,
    local_grad,
    weights_buf,
    gate_part,
    gate_send,
    gate_got,
    load_sems,
    send_sems,
    recv_sems,
):
    me = lax.axis_index("mem")
    stored, rows, width = mk_hbm.shape
    query_count = pk_hbm.shape[0]
    dim = width // head_count
    scale = dim**-0.5
    cap = 2
    peers = mem_count - 1

    barrier = pltpu.get_barrier_semaphore()

    def greet(step, _):
        pl.semaphore_signal(
            barrier, inc=1, device_id={"mem": peer_of(step, me, mem_count)}, device_id_type=MESH
        )
        return 0

    lax.fori_loop(1, mem_count, greet, 0)

    table_rows = stored + query_count

    def load_table(source, table, offset, which):
        count = source.shape[0]

        def body(h, _):
            pltpu.make_async_copy(
                source.at[:, :, pl.ds(pl.multiple_of(h * dim, dim), dim)],
                table.at[pl.ds(h * table_rows + offset, count)],
                load_sems.at[which],
            ).start()
            return 0

        lax.fori_loop(0, head_count, body, 0)

    def await_table(source, table, which):
        whole = table.at[pl.ds(0, head_count * source.shape[0])]
        pltpu.make_async_copy(whole, whole, load_sems.at[which]).wait()

    load_table(mk_hbm, k_table, 0, 0)
    load_table(pk_hbm, k_table, stored, 1)
    load_table(mv_hbm, v_table, 0, 2)
    load_table(pv_hbm, v_table, stored, 3)
    loads = [
        pltpu.make_async_copy(q_hbm, q_buf, load_sems.at[4]),
        pltpu.make_async_copy(g_hbm, g_buf, load_sems.at[5]),
    ]
    for load in loads:
        load.start()
    code_got[me] = codes_ref[me]

    pl.semaphore_wait(barrier, peers)

    def remote(src, dst, which, device):
        return pltpu.make_async_remote_copy(
            src_ref=src,
            dst_ref=dst,
            send_sem=send_sems.at[which],
            recv_sem=recv_sems.at[which],
            device_id={"mem": device},
            device_id_type=MESH,
        )

    def send_codes(step, _):
        device = peer_of(step, me, mem_count)
        remote(codes_ref.at[device], code_got.at[me], 0, device).start()
        return 0

    lax.fori_loop(1, mem_count, send_codes, 0)

    following = lax.rem(me + 1, mem_count)
    halo_k = remote(pk_hbm.at[query_count - 1], halo.at[0], 1, following)
    halo_v = remote(pv_hbm.at[query_count - 1], halo.at[1], 2, following)
    halo_k.start()
    halo_v.start()

    some = pl.ds(0, peers)
    remote(codes_ref.at[some], code_got.at[some], 0, following).wait()
    code_copy = pltpu.make_async_copy(code_got, code_smem, load_sems.at[6])
    code_copy.start()
    await_table(mk_hbm, k_table, 0)
    await_table(pk_hbm, k_table, 1)
    await_table(mv_hbm, v_table, 2)
    await_table(pv_hbm, v_table, 3)
    code_copy.wait()

    def gather(table, device, out, at):
        for rank in range(cap):
            out[at + rank] = table[place_ref[code_smem[device, 0, rank]]]

    def serve(table, out, got, which):
        gather(table, peer_of(1, me, mem_count), out, cap)

        def send(step):
            device = peer_of(step, me, mem_count)
            remote(
                out.at[pl.ds(step * cap, cap)], got.at[pl.ds(me * cap, cap)], which, device
            ).start()

        def body(step, _):
            gather(table, peer_of(step, me, mem_count), out, step * cap)
            send(step - 1)
            return 0

        lax.fori_loop(2, mem_count, body, 0)
        gather(table, me, got, me * cap)
        send(peers)

    serve(k_table, k_send, k_got, 3)
    serve(v_table, v_send, v_got, 4)

    for load in loads:
        load.wait()
    halo_k.wait()
    halo_v.wait()

    first = me == 0

    def places(b, h):
        return pl.ds(b * rows, rows), pl.ds(pl.multiple_of(h * dim, dim), dim)

    def mix_of(h):
        return 1.0 / (1.0 + jnp.exp(-jnp.full((1, dim), gate_ref[h], jnp.float32)))

    def local_head(h, _):
        columns = pl.ds(pl.multiple_of(h * dim, dim), dim)
        own = h * table_rows + stored
        rest = 1.0 - mix_of(h)
        part = jnp.zeros((1, dim), jnp.float32)
        for b in range(query_count):
            at = places(b, h)
            q, g = q_buf[at], g_buf[at]
            if b == 0:
                older_k, older_v = halo[0, :, columns], halo[1, :, columns]
            else:
                older_k, older_v = k_table[own + b - 1], v_table[own + b - 1]
            keys = jnp.concatenate([older_k, k_table[own + b]], axis=0)
            values = jnp.concatenate([older_v, v_table[own + b]], axis=0)
            raw = across(q, keys)
            if b == 0:
                column_ids = lax.broadcasted_iota(jnp.int32, raw.shape, 1)
                raw = jnp.where(first & (column_ids < rows), -jnp.inf, raw)
            weights = softmax(raw, scale)
            result = onto(weights.astype(jnp.bfloat16), values)
            weight_grad = across(g, values)
            inner = jnp.sum(weights * weight_grad, axis=-1, keepdims=True)
            score_grad = weights * (weight_grad - inner) * rest[:, :1]
            local_grad[at] = onto(score_grad.astype(jnp.bfloat16), keys)
            local_out[at] = result * rest
            part = part - jnp.sum(g.astype(jnp.float32) * result, axis=0, keepdims=True)
        gate_part[h] = part
        return 0

    lax.fori_loop(0, head_count, local_head, 0)

    def blocks(got, b, h):
        first_item = (b * head_count + h) * pick_count
        return jnp.concatenate([got[where_ref[first_item + k]] for k in range(pick_count)], axis=0)

    everyone = pl.ds(0, peers * cap)
    remote(k_send.at[everyone], k_got.at[everyone], 3, following).wait()

    def memory_weights(h, _):
        for b in range(query_count):
            raw = across(q_buf[places(b, h)], blocks(k_got, b, h))
            weights_buf[b * head_count + h] = softmax(raw, scale)
        return 0

    lax.fori_loop(0, head_count, memory_weights, 0)

    remote(v_send.at[everyone], v_got.at[everyone], 4, following).wait()

    def memory_result(h, _):
        mix = mix_of(h)
        part = gate_part[h]
        for b in range(query_count):
            at = places(b, h)
            weights = weights_buf[b * head_count + h].astype(jnp.bfloat16)
            result = onto(weights, blocks(v_got, b, h))
            att_ref[at] = (mix * result + local_out[at]).astype(jnp.bfloat16)
            part = part + jnp.sum(g_buf[at].astype(jnp.float32) * result, axis=0, keepdims=True)
        gate_part[h] = part
        return 0

    lax.fori_loop(0, head_count, memory_result, 0)

    lane_ids = lax.broadcasted_iota(jnp.int32, (1, dim), 1)
    total = jnp.zeros((1, dim), jnp.float32)
    for h in range(head_count):
        mix = mix_of(h)
        term = jnp.sum(gate_part[h], axis=-1, keepdims=True) * (mix * (1.0 - mix))
        total = jnp.where(lane_ids == h, term, total)
    gate_send[...] = total
    gate_got[me] = total

    def memory_grad(h, _):
        mix = mix_of(h)
        for b in range(query_count):
            at = places(b, h)
            weights = weights_buf[b * head_count + h]
            weight_grad = across(g_buf[at], blocks(v_got, b, h))
            inner = jnp.sum(weights * weight_grad, axis=-1, keepdims=True)
            score_grad = weights * (weight_grad - inner) * mix[:, :1]
            grad = onto(score_grad.astype(jnp.bfloat16), blocks(k_got, b, h))
            qg_ref[at] = ((grad + local_grad[at]) * scale).astype(jnp.bfloat16)
        return 0

    memory_grad(0, 0)

    def send_gate(step, _):
        device = peer_of(step, me, mem_count)
        remote(gate_send, gate_got.at[me], 5, device).start()
        return 0

    lax.fori_loop(1, mem_count, send_gate, 0)
    lax.fori_loop(1, head_count, memory_grad, 0)

    arrived = remote(gate_got.at[some], gate_got.at[some], 5, following)
    arrived.wait()
    gate_out_ref[...] = jnp.sum(gate_got[...], axis=0)


def local(
    queries,
    grad_out,
    mem_keys,
    mem_values,
    prev_keys,
    prev_values,
    gate_logit,
    location,
    top_blocks,
    write_slot,
):
    mem_count = lax.axis_size("mem")
    query_count, head_count, pick_count = top_blocks.shape
    stored, block_rows, row_width = mem_keys.shape
    dim = row_width // head_count
    cap = 2
    owner_ids, position, code_ids, is_live = route_table(top_blocks, location, stored)
    target = jnp.where(is_live, owner_ids * dim + position, mem_count * dim)
    codes = jnp.zeros((mem_count * dim,), jnp.int32).at[target].set(code_ids, mode="drop")
    codes = codes.reshape(mem_count, 1, dim)
    where = owner_ids * cap + position
    place = jnp.arange(stored, dtype=jnp.int32)
    for i in range(query_count):
        place = jnp.where(jnp.arange(stored) == write_slot[i], stored + i, place)
    table_rows = stored + query_count
    place = (jnp.arange(head_count, dtype=jnp.int32)[:, None] * table_rows + place).reshape(-1)
    any_space = pl.BlockSpec(memory_space=pl.ANY)
    smem = pl.BlockSpec(memory_space=pltpu.SMEM)
    vmem = pl.BlockSpec(memory_space=pltpu.VMEM)
    items = mem_count * cap
    attended, query_grad, gate = pl.pallas_call(
        functools.partial(kernel, mem_count, head_count, pick_count),
        out_shape=(
            jax.ShapeDtypeStruct(queries.shape, jnp.bfloat16),
            jax.ShapeDtypeStruct(queries.shape, jnp.bfloat16),
            jax.ShapeDtypeStruct((1, dim), jnp.float32),
        ),
        in_specs=[any_space] * 6 + [vmem, smem, smem, smem],
        out_specs=(vmem, vmem, vmem),
        scratch_shapes=[
            pltpu.VMEM(queries.shape, jnp.bfloat16),
            pltpu.VMEM(queries.shape, jnp.bfloat16),
            pltpu.VMEM((head_count * table_rows, block_rows, dim), jnp.bfloat16),
            pltpu.VMEM((head_count * table_rows, block_rows, dim), jnp.bfloat16),
            pltpu.VMEM((2, block_rows, row_width), jnp.bfloat16),
            pltpu.VMEM((items, block_rows, dim), jnp.bfloat16),
            pltpu.VMEM((items, block_rows, dim), jnp.bfloat16),
            pltpu.VMEM((items, block_rows, dim), jnp.bfloat16),
            pltpu.VMEM((items, block_rows, dim), jnp.bfloat16),
            pltpu.VMEM((mem_count, 1, dim), jnp.int32),
            pltpu.SMEM((mem_count, 1, dim), jnp.int32),
            pltpu.VMEM(queries.shape, jnp.float32),
            pltpu.VMEM(queries.shape, jnp.float32),
            pltpu.VMEM(
                (query_count * head_count, block_rows, pick_count * block_rows), jnp.float32
            ),
            pltpu.VMEM((head_count, 1, dim), jnp.float32),
            pltpu.VMEM((1, dim), jnp.float32),
            pltpu.VMEM((mem_count, 1, dim), jnp.float32),
            pltpu.SemaphoreType.DMA((7,)),
            pltpu.SemaphoreType.DMA((6,)),
            pltpu.SemaphoreType.DMA((6,)),
        ],
        compiler_params=pltpu.CompilerParams(
            collective_id=0, has_side_effects=True, vmem_limit_bytes=60 * 2**20
        ),
        name="retrieve_attend",
    )(
        queries,
        grad_out,
        mem_keys,
        mem_values,
        prev_keys,
        prev_values,
        codes,
        where,
        place,
        gate_logit,
    )
    return (attended, query_grad, gate[0, :head_count])


def solution(mesh):
    in_specs = (
        P(("doc", "mem"), None),
        P(("doc", "mem"), None),
        P(("doc", "mem"), None, None),
        P(("doc", "mem"), None, None),
        P(("doc", "mem"), None, None),
        P(("doc", "mem"), None, None),
        P(),
        P("doc"),
        P(("doc", "mem"), None, None),
        P(("doc", "mem")),
    )
    out_specs = (P(("doc", "mem"), None), P(("doc", "mem"), None), P("doc"))
    return jax.shard_map(local, mesh=mesh, in_specs=in_specs, out_specs=out_specs, check_vma=False)
```

time: 384 us -> 242 us (0.63)
  Pallas kernels: 0 us -> 227 us
  waiting for transfers between devices: 162 us -> 0 us
  local copies, waits for them, and re-layouts: 75.4 us -> 11.5 us
  starting transfers between devices: 61.6 us -> 0 us
  matrix products: 53.3 us -> 0 us
  other arithmetic: 29 us -> 2.49 us
    pallas_call x0 -> x1, Pallas kernels: none -> 227 us  [local(): pl.pallas_call(functools.partial(kernel, mem_count, head_count, pick_coun...]
    all_to_all x3 -> x0, waiting for transfers between devices: 162 us -> none  [the longest x1 154 us: sent_together(): lax.all_to_all(both, axis, split_axis=split_dim, concat_axis=concat_dim,...]
    all_to_all x3 -> x0, starting transfers between devices: 55.4 us -> none  [the longest x1 32.6 us: copy_for_each(): lax.all_to_all(jnp.broadcast_to(x[None], (length, *x.shape)), axis, 0, 0,...]
    dot_general x8 -> x0, matrix products: 53.3 us -> none  [the longest x2 23.5 us: attend_blocks(): jnp.einsum('nhqk,nhkd->nhqd', score_grad, key_rows, preferred_element_typ...]
    gather x4 -> x0, local copies, waits for them, and re-layouts: 18.6 us -> none  [the longest x1 5.35 us: local(): fetched_keys[owner_ids, position]]
    reshape x6 -> x0, local copies, waits for them, and re-layouts: 16.3 us -> none  [head_major(): blocks.reshape(block_count, row_count, head_count, row_width // head_count)]
    unnamed x33 -> x5, local copies, waits for them, and re-layouts: 20 us -> 5.38 us
    concatenate x4 -> x0, other arithmetic: 11.9 us -> none  [the longest x1 7.4 us: sent_together(): both = jnp.concatenate(arrays, axis=along)]
  transfers between devices with their start and end apart: 5 -> 0, of which waited for: 2 -> 0; matrix products, arithmetic and copies ran while one was open for 14% -> 0% of each run, Pallas kernels for 0% -> 0%
where the time goes in v1:
time: 242 us; the launch traced here: 241 us
  Pallas kernels  227 us (94%)
  local copies, waits for them, and re-layouts  11.5 us (5%)
  other arithmetic  2.49 us (1%)
    pallas_call x1, Pallas kernels, local(): pl.pallas_call(functools.partial(kernel, mem_count, head_count, pick_coun...  227 us
    unnamed x5, local copies, waits for them, and re-layouts  5.38 us

profile of v1, /device:TPU:6, one launch (start us, length us, event | category | flops | bytes accessed | tf_op | source)
XLA Modules:
  0.0 241.3 jit_solution(10093868762730041461)
XLA Ops:
  0.6 0.0 copy-start
  0.7 1.3 fusion.9
  2.0 1.3 compare_select_fusion.6
  3.3 0.1 broadcast_add_fusion
  3.3 0.6 add.151.place_ref
  4.0 0.8 copy.17
  4.7 0.1 reshape.257
  4.8 0.1 reshape.256
  5.0 0.0 copy-done
  5.0 1.3 gather_fusion
  6.3 0.2 fusion.1
  6.5 0.2 convert_reduce_fusion
  6.7 0.2 select_reduce_fusion
  6.9 0.5 multiply_add_fusion.where_ref
  7.4 1.6 scatter_custom_fusion
  9.0 226.6 %retrieve_attend.1 = (bf16[256,2048]{1,0:T(8,128)(2,1)}, bf16[256,2048]{1,0:T(8,128)(2,1)}, f32[1,128]{1,0:T(1,128)}) custom-call(bf16[256,2048]{1,0:T(8,128)(2,1)} %q_hbm.1, bf16[256,2048]{1,0:T(8,128)(2,1)} %g_hbm.1, bf16[6,128,2048]{2,1,0:T(8,128)(2,1)} %mk_hbm.1, bf16[6,128,2048]{2,1,0:T(8,128)(2,1)} %mv_hbm.1, bf16[2,128,2048]{2,1,0:T(8,128)(2,1)} %pk_hbm.1, ...), custom_call_target="tpu_custom_call" | custom-call | tf_op jit(solution)/shard_map/retrieve_attend/pallas_call | solution.py:350
  235.6 1.1 slice_bitcast_fusion
  236.7 2.3 copy.21
  239.0 2.3 copy.22
  (7 shorter events, 0.1 us)
Async XLA Ops:
  0.6 4.3 %copy-start = (s32[384]{0:T(512)S(1)}, s32[384]{0:T(512)}, u32[]{:S(2)}) copy-start(s32[384]{0:T(512)} %param.17) | copy-start | bytes 4612

commit v2 on v1

--- a/solution.py
+++ b/solution.py
@@ -13,22 +13,58 @@
 LOG2_E = 1.4426950408889634
 
 
-def route_table(top_blocks, location, stored):
-    query_count, head_count, pick_count = top_blocks.shape
-    item_count = query_count * head_count * pick_count
-    slot_ids = jnp.take(location, top_blocks.reshape(item_count), axis=0)
-    owner_ids = slot_ids // stored
-    item_ids = jnp.arange(item_count, dtype=jnp.int32)
-    head_ids = item_ids // pick_count % head_count
-    code_ids = head_ids * stored + slot_ids % stored
-    earlier = item_ids[None, :] < item_ids[:, None]
-    same_owner = owner_ids[:, None] == owner_ids[None, :]
-    pair_ids = slot_ids * head_count + head_ids
-    same_pair = pair_ids[:, None] == pair_ids[None, :]
-    leading = jnp.logical_not(jnp.any(same_pair & earlier, axis=1))
-    lead_rank = jnp.sum(same_owner & earlier & leading[None, :], axis=1)
-    position = jnp.sum(jnp.where(same_pair & leading[None, :], lead_rank[None, :], 0), axis=1)
-    return (owner_ids, position, code_ids, leading)
+def route(top_ref, location_ref, write_ref, mem_count, head_count, stored, cap):
+    query_count, _, pick_count = top_ref.shape
+    items = query_count * head_count * pick_count
+    lane = lax.broadcasted_iota(jnp.int32, (1, items), 1)
+
+    def slots_of(h, slots):
+        for b in range(query_count):
+            for k in range(pick_count):
+                item = (b * head_count + h) * pick_count + k
+                slots = jnp.where(lane == item, location_ref[top_ref[b, h, k]], slots)
+        return slots
+
+    slots = lax.fori_loop(0, head_count, slots_of, jnp.zeros((1, items), jnp.int32))
+
+    def split(value):
+        quotient = lax.shift_right_logical(value * ((1 << 18) // stored + 1), 18)
+        return quotient, value - quotient * stored
+
+    owners, inside = split(slots)
+    heads = lax.shift_right_logical(lane, pick_count.bit_length() - 1) & (head_count - 1)
+    codes = heads * stored + inside
+    pairs = slots * head_count + heads
+    square = (items, items)
+    pair_row = jnp.broadcast_to(pairs, square)
+    owner_row = jnp.broadcast_to(owners, square)
+    same_pair = pair_row == pair_row.T
+    same_owner = owner_row == owner_row.T
+    row = lax.broadcasted_iota(jnp.int32, square, 0)
+    column = lax.broadcasted_iota(jnp.int32, square, 1)
+
+    def count(condition, axis):
+        return jnp.sum(jnp.where(condition, 1, 0), axis=axis, keepdims=True)
+
+    lead_of_row = count(same_pair & (column < row), 1) == 0
+    lead_of_column = count(same_pair & (row < column), 0) == 0
+    rank_of_row = count(same_owner & (column < row) & lead_of_column, 1)
+    position = jnp.sum(
+        jnp.where(same_pair & lead_of_row, rank_of_row, 0), axis=0, keepdims=True
+    )
+    asked_shape = (mem_count, items)
+    owner = lax.broadcasted_iota(jnp.int32, asked_shape, 0)
+    asked_lane = lax.broadcasted_iota(jnp.int32, asked_shape, 1)
+    asked = jnp.zeros(asked_shape, jnp.int32)
+    for rank in range(cap):
+        match = (owners == owner) & lead_of_column & (position == rank)
+        code = jnp.sum(jnp.where(match, codes, 0), axis=1, keepdims=True)
+        asked = jnp.where(asked_lane == rank, code, asked)
+    head, slot = split(lane)
+    place = slot
+    for i in range(query_count):
+        place = jnp.where(slot == write_ref[i], stored + i, place)
+    return asked, owners * cap + position, head * (stored + query_count) + place
 
 
 def peer_of(step, me, mem_count):
@@ -68,9 +104,9 @@
     mv_hbm,
     pk_hbm,
     pv_hbm,
-    codes_ref,
-    where_ref,
-    place_ref,
+    top_ref,
+    location_ref,
+    write_ref,
     gate_ref,
     att_ref,
     qg_ref,
@@ -84,8 +120,11 @@
     v_send,
     k_got,
     v_got,
+    codes_ref,
     code_got,
     code_smem,
+    spots,
+    spots_smem,
     local_out,
     local_grad,
     weights_buf,
@@ -143,6 +182,13 @@
     ]
     for load in loads:
         load.start()
+    asked, where, place = route(
+        top_ref, location_ref, write_ref, mem_count, head_count, stored, cap
+    )
+    for device in range(mem_count):
+        codes_ref[device] = asked[device : device + 1, :]
+    spots[0] = where
+    spots[1] = place
     code_got[me] = codes_ref[me]
 
     pl.semaphore_wait(barrier, peers)
@@ -163,6 +209,8 @@
         return 0
 
     lax.fori_loop(1, mem_count, send_codes, 0)
+    spots_copy = pltpu.make_async_copy(spots, spots_smem, load_sems.at[7])
+    spots_copy.start()
 
     following = lax.rem(me + 1, mem_count)
     halo_k = remote(pk_hbm.at[query_count - 1], halo.at[0], 1, following)
@@ -179,10 +227,11 @@
     await_table(mv_hbm, v_table, 2)
     await_table(pv_hbm, v_table, 3)
     code_copy.wait()
+    spots_copy.wait()
 
     def gather(table, device, out, at):
         for rank in range(cap):
-            out[at + rank] = table[place_ref[code_smem[device, 0, rank]]]
+            out[at + rank] = table[spots_smem[1, 0, code_smem[device, 0, rank]]]
 
     def serve(table, out, got, which):
         gather(table, peer_of(1, me, mem_count), out, cap)
@@ -251,7 +300,7 @@
 
     def blocks(got, b, h):
         first_item = (b * head_count + h) * pick_count
-        return jnp.concatenate([got[where_ref[first_item + k]] for k in range(pick_count)], axis=0)
+        return jnp.concatenate([got[spots_smem[0, 0, first_item + k]] for k in range(pick_count)], axis=0)
 
     everyone = pl.ds(0, peers * cap)
     remote(k_send.at[everyone], k_got.at[everyone], 3, following).wait()
@@ -314,6 +363,18 @@
     arrived = remote(gate_got.at[some], gate_got.at[some], 5, following)
     arrived.wait()
     gate_out_ref[...] = jnp.sum(gate_got[...], axis=0)
+
+
+def publish(att_ref, qg_ref, gate_ref, att_hbm, qg_hbm, gate_out, sems):
+    copies = [
+        pltpu.make_async_copy(att_ref, att_hbm, sems.at[0]),
+        pltpu.make_async_copy(qg_ref, qg_hbm, sems.at[1]),
+    ]
+    for copy in copies:
+        copy.start()
+    gate_out[...] = gate_ref[0, : gate_out.shape[0]]
+    for copy in copies:
+        copy.wait()
 
 
 def local(
@@ -333,16 +394,7 @@
     stored, block_rows, row_width = mem_keys.shape
     dim = row_width // head_count
     cap = 2
-    owner_ids, position, code_ids, is_live = route_table(top_blocks, location, stored)
-    target = jnp.where(is_live, owner_ids * dim + position, mem_count * dim)
-    codes = jnp.zeros((mem_count * dim,), jnp.int32).at[target].set(code_ids, mode="drop")
-    codes = codes.reshape(mem_count, 1, dim)
-    where = owner_ids * cap + position
-    place = jnp.arange(stored, dtype=jnp.int32)
-    for i in range(query_count):
-        place = jnp.where(jnp.arange(stored) == write_slot[i], stored + i, place)
     table_rows = stored + query_count
-    place = (jnp.arange(head_count, dtype=jnp.int32)[:, None] * table_rows + place).reshape(-1)
     any_space = pl.BlockSpec(memory_space=pl.ANY)
     smem = pl.BlockSpec(memory_space=pltpu.SMEM)
     vmem = pl.BlockSpec(memory_space=pltpu.VMEM)
@@ -350,11 +402,11 @@
     attended, query_grad, gate = pl.pallas_call(
         functools.partial(kernel, mem_count, head_count, pick_count),
         out_shape=(
-            jax.ShapeDtypeStruct(queries.shape, jnp.bfloat16),
-            jax.ShapeDtypeStruct(queries.shape, jnp.bfloat16),
-            jax.ShapeDtypeStruct((1, dim), jnp.float32),
+            pltpu.VMEM(queries.shape, jnp.bfloat16),
+            pltpu.VMEM(queries.shape, jnp.bfloat16),
+            pltpu.VMEM((1, dim), jnp.float32),
         ),
-        in_specs=[any_space] * 6 + [vmem, smem, smem, smem],
+        in_specs=[any_space] * 6 + [smem] * 4,
         out_specs=(vmem, vmem, vmem),
         scratch_shapes=[
             pltpu.VMEM(queries.shape, jnp.bfloat16),
@@ -367,7 +419,10 @@
             pltpu.VMEM((items, block_rows, dim), jnp.bfloat16),
             pltpu.VMEM((items, block_rows, dim), jnp.bfloat16),
             pltpu.VMEM((mem_count, 1, dim), jnp.int32),
+            pltpu.VMEM((mem_count, 1, dim), jnp.int32),
             pltpu.SMEM((mem_count, 1, dim), jnp.int32),
+            pltpu.VMEM((2, 1, dim), jnp.int32),
+            pltpu.SMEM((2, 1, dim), jnp.int32),
             pltpu.VMEM(queries.shape, jnp.float32),
             pltpu.VMEM(queries.shape, jnp.float32),
             pltpu.VMEM(
@@ -376,7 +431,7 @@
             pltpu.VMEM((head_count, 1, dim), jnp.float32),
             pltpu.VMEM((1, dim), jnp.float32),
             pltpu.VMEM((mem_count, 1, dim), jnp.float32),
-            pltpu.SemaphoreType.DMA((7,)),
+            pltpu.SemaphoreType.DMA((8,)),
             pltpu.SemaphoreType.DMA((6,)),
             pltpu.SemaphoreType.DMA((6,)),
         ],
@@ -391,12 +446,23 @@
         mem_values,
         prev_keys,
         prev_values,
-        codes,
-        where,
-        place,
+        top_blocks,
+        location,
+        write_slot,
         gate_logit,
     )
-    return (attended, query_grad, gate[0, :head_count])
+    return pl.pallas_call(
+        publish,
+        out_shape=(
+            jax.ShapeDtypeStruct(queries.shape, jnp.bfloat16),
+            jax.ShapeDtypeStruct(queries.shape, jnp.bfloat16),
+            jax.ShapeDtypeStruct((head_count,), jnp.float32),
+        ),
+        in_specs=[vmem] * 3,
+        out_specs=(any_space, any_space, vmem),
+        scratch_shapes=[pltpu.SemaphoreType.DMA((2,))],
+        name="publish",
+    )(*(pltpu.with_memory_space_constraint(x, pltpu.VMEM) for x in (attended, query_grad, gate)))
 
 
 def solution(mesh):

time: 242 us -> 230 us (0.950)
  local copies, waits for them, and re-layouts: 11.5 us -> 1.37 us
  other arithmetic: 2.49 us -> 0 us
    unnamed x5 -> x1, local copies, waits for them, and re-layouts: 5.38 us -> 1.37 us
where the time goes in v2:
time: 230 us; the launch traced here: 229 us
  Pallas kernels  227 us (99%)
    pallas_call x1, Pallas kernels, local(): pl.pallas_call(functools.partial(kernel, mem_count, head_count, pick_coun...  225 us

profile of v2, /device:TPU:6, one launch (start us, length us, event | category | flops | bytes accessed | tf_op | source)
XLA Modules:
  0.0 229.3 jit_solution(7594987784597812644)
XLA Ops:
  0.6 1.4 copy.13.top_ref
  2.0 225.4 %retrieve_attend.1 = (bf16[256,2048]{1,0:T(8,128)(2,1)S(1)}, bf16[256,2048]{1,0:T(8,128)(2,1)S(1)}, f32[1,128]{1,0:T(1,128)S(1)}) custom-call(bf16[256,2048]{1,0:T(8,128)(2,1)} %q_hbm.1, bf16[256,2048]{1,0:T(8,128)(2,1)} %g_hbm.1, bf16[6,128,2048]{2,1,0:T(8,128)(2,1)} %mk_hbm.1, bf16[6,128,2048]{2,1,0:T(8,128)(2,1)} %mv_hbm.1, bf16[2,128,2048]{2,1,0:T(8,128)(2,1)} %pk_hbm.1, ...), custom_call_target="tpu_custom_call" | custom-call | tf_op jit(solution)/shard_map/retrieve_attend/pallas_call | solution.py:402
  227.4 1.8 publish.1

commit v3 on v2

--- a/solution.py
+++ b/solution.py
@@ -14,7 +14,7 @@
 
 
 def route(top_ref, location_ref, write_ref, mem_count, head_count, stored, cap):
-    query_count, _, pick_count = top_ref.shape
+    query_count, pick_count, _ = top_ref.shape
     items = query_count * head_count * pick_count
     lane = lax.broadcasted_iota(jnp.int32, (1, items), 1)
 
@@ -22,7 +22,7 @@
         for b in range(query_count):
             for k in range(pick_count):
                 item = (b * head_count + h) * pick_count + k
-                slots = jnp.where(lane == item, location_ref[top_ref[b, h, k]], slots)
+                slots = jnp.where(lane == item, location_ref[top_ref[b, k, h]], slots)
         return slots
 
     slots = lax.fori_loop(0, head_count, slots_of, jnp.zeros((1, items), jnp.int32))
@@ -128,6 +128,7 @@
     local_out,
     local_grad,
     weights_buf,
+    mixed_buf,
     gate_part,
     gate_send,
     gate_got,
@@ -306,28 +307,33 @@
     remote(k_send.at[everyone], k_got.at[everyone], 3, following).wait()
 
     def memory_weights(h, _):
+        mix = mix_of(h)[:, :1]
         for b in range(query_count):
             raw = across(q_buf[places(b, h)], blocks(k_got, b, h))
-            weights_buf[b * head_count + h] = softmax(raw, scale)
+            weights = softmax(raw, scale)
+            weights_buf[b * head_count + h] = weights.astype(jnp.bfloat16)
+            mixed_buf[b * head_count + h] = weights * mix
         return 0
 
     lax.fori_loop(0, head_count, memory_weights, 0)
 
     remote(v_send.at[everyone], v_got.at[everyone], 4, following).wait()
 
-    def memory_result(h, _):
-        mix = mix_of(h)
-        part = gate_part[h]
-        for b in range(query_count):
-            at = places(b, h)
-            weights = weights_buf[b * head_count + h].astype(jnp.bfloat16)
-            result = onto(weights, blocks(v_got, b, h))
-            att_ref[at] = (mix * result + local_out[at]).astype(jnp.bfloat16)
-            part = part + jnp.sum(g_buf[at].astype(jnp.float32) * result, axis=0, keepdims=True)
-        gate_part[h] = part
-        return 0
-
-    lax.fori_loop(0, head_count, memory_result, 0)
+    def memory_result(step, _):
+        for h in (step * 2, step * 2 + 1):
+            mix = mix_of(h)
+            part = gate_part[h]
+            for b in range(query_count):
+                at = places(b, h)
+                result = onto(weights_buf[b * head_count + h], blocks(v_got, b, h))
+                att_ref[at] = (mix * result + local_out[at]).astype(jnp.bfloat16)
+                part = part + jnp.sum(
+                    g_buf[at].astype(jnp.float32) * result, axis=0, keepdims=True
+                )
+            gate_part[h] = part
+        return 0
+
+    lax.fori_loop(0, head_count // 2, memory_result, 0)
 
     lane_ids = lax.broadcasted_iota(jnp.int32, (1, dim), 1)
     total = jnp.zeros((1, dim), jnp.float32)
@@ -338,19 +344,18 @@
     gate_send[...] = total
     gate_got[me] = total
 
-    def memory_grad(h, _):
-        mix = mix_of(h)
-        for b in range(query_count):
-            at = places(b, h)
-            weights = weights_buf[b * head_count + h]
-            weight_grad = across(g_buf[at], blocks(v_got, b, h))
-            inner = jnp.sum(weights * weight_grad, axis=-1, keepdims=True)
-            score_grad = weights * (weight_grad - inner) * mix[:, :1]
-            grad = onto(score_grad.astype(jnp.bfloat16), blocks(k_got, b, h))
-            qg_ref[at] = ((grad + local_grad[at]) * scale).astype(jnp.bfloat16)
-        return 0
-
-    memory_grad(0, 0)
+    def memory_grad(step, _):
+        for h in (step * 2, step * 2 + 1):
+            less = 1.0 + jnp.exp(-jnp.full((1, 1), gate_ref[h], jnp.float32))
+            for b in range(query_count):
+                at = places(b, h)
+                mixed = mixed_buf[b * head_count + h]
+                weight_grad = across(g_buf[at], blocks(v_got, b, h))
+                inner = jnp.sum(mixed * weight_grad, axis=-1, keepdims=True) * less
+                score_grad = (mixed * (weight_grad - inner)).astype(jnp.bfloat16)
+                grad = onto(score_grad, blocks(k_got, b, h))
+                qg_ref[at] = ((grad + local_grad[at]) * scale).astype(jnp.bfloat16)
+        return 0
 
     def send_gate(step, _):
         device = peer_of(step, me, mem_count)
@@ -358,7 +363,7 @@
         return 0
 
     lax.fori_loop(1, mem_count, send_gate, 0)
-    lax.fori_loop(1, head_count, memory_grad, 0)
+    lax.fori_loop(0, head_count // 2, memory_grad, 0)
 
     arrived = remote(gate_got.at[some], gate_got.at[some], 5, following)
     arrived.wait()
@@ -399,6 +404,7 @@
     smem = pl.BlockSpec(memory_space=pltpu.SMEM)
     vmem = pl.BlockSpec(memory_space=pltpu.VMEM)
     items = mem_count * cap
+    weights_shape = (query_count * head_count, block_rows, pick_count * block_rows)
     attended, query_grad, gate = pl.pallas_call(
         functools.partial(kernel, mem_count, head_count, pick_count),
         out_shape=(
@@ -425,9 +431,8 @@
             pltpu.SMEM((2, 1, dim), jnp.int32),
             pltpu.VMEM(queries.shape, jnp.float32),
             pltpu.VMEM(queries.shape, jnp.float32),
-            pltpu.VMEM(
-                (query_count * head_count, block_rows, pick_count * block_rows), jnp.float32
-            ),
+            pltpu.VMEM(weights_shape, jnp.bfloat16),
+            pltpu.VMEM(weights_shape, jnp.float32),
             pltpu.VMEM((head_count, 1, dim), jnp.float32),
             pltpu.VMEM((1, dim), jnp.float32),
             pltpu.VMEM((mem_count, 1, dim), jnp.float32),
@@ -446,7 +451,7 @@
         mem_values,
         prev_keys,
         prev_values,
-        top_blocks,
+        jnp.transpose(top_blocks, (0, 2, 1)),
         location,
         write_slot,
         gate_logit,

time: 230 us -> 226 us (0.983)
    pallas_call x1, Pallas kernels: 225 us -> 223 us  [local(): pl.pallas_call(functools.partial(kernel, mem_count, head_count, pick_coun...]
where the time goes in v3:
time: 226 us; the launch traced here: 225 us
  Pallas kernels  225 us (100%)
    pallas_call x1, Pallas kernels, local(): pl.pallas_call(functools.partial(kernel, mem_count, head_count, pick_coun...  223 us

profile of v3, /device:TPU:6, one launch (start us, length us, event | category | flops | bytes accessed | tf_op | source)
XLA Modules:
  0.0 225.3 jit_solution(7685190092723247527)
XLA Ops:
  0.6 222.8 %retrieve_attend.1 = (bf16[256,2048]{1,0:T(8,128)(2,1)S(1)}, bf16[256,2048]{1,0:T(8,128)(2,1)S(1)}, f32[1,128]{1,0:T(1,128)S(1)}) custom-call(bf16[256,2048]{1,0:T(8,128)(2,1)} %q_hbm.1, bf16[256,2048]{1,0:T(8,128)(2,1)} %g_hbm.1, bf16[6,128,2048]{2,1,0:T(8,128)(2,1)} %mk_hbm.1, bf16[6,128,2048]{2,1,0:T(8,128)(2,1)} %mv_hbm.1, bf16[2,128,2048]{2,1,0:T(8,128)(2,1)} %pk_hbm.1, ...), custom_call_target="tpu_custom_call" | custom-call | tf_op jit(solution)/shard_map/retrieve_attend/pallas_call | solution.py:408
  223.5 1.8 publish.1

commit v4 on v3

--- a/solution.py
+++ b/solution.py
@@ -78,6 +78,23 @@
     return (lax.rem(y + dy, y_chips) * Z_CHIPS + lax.rem(z + dz, Z_CHIPS)) * CORES + lax.rem(
         c + dc, CORES
     )
+
+
+def far_first(mem_count, visit):
+    turns = mem_count // Z_CHIPS
+
+    def group(places, first_turn):
+        def body(turn, _):
+            for place in places:
+                visit(turn * Z_CHIPS + place + 1)
+            return 0
+
+        lax.fori_loop(first_turn, turns, body, 0)
+
+    group((0, 1, 2), 0)
+    group((3, 4), 0)
+    group((5, 6), 0)
+    group((-1,), 1)
 
 
 def across(a, b):
@@ -146,13 +163,12 @@
 
     barrier = pltpu.get_barrier_semaphore()
 
-    def greet(step, _):
+    def greet(step):
         pl.semaphore_signal(
             barrier, inc=1, device_id={"mem": peer_of(step, me, mem_count)}, device_id_type=MESH
         )
-        return 0
-
-    lax.fori_loop(1, mem_count, greet, 0)
+
+    far_first(mem_count, greet)
 
     table_rows = stored + query_count
 
@@ -204,12 +220,11 @@
             device_id_type=MESH,
         )
 
-    def send_codes(step, _):
+    def send_codes(step):
         device = peer_of(step, me, mem_count)
         remote(codes_ref.at[device], code_got.at[me], 0, device).start()
-        return 0
-
-    lax.fori_loop(1, mem_count, send_codes, 0)
+
+    far_first(mem_count, send_codes)
     spots_copy = pltpu.make_async_copy(spots, spots_smem, load_sems.at[7])
     spots_copy.start()
 
@@ -357,12 +372,11 @@
                 qg_ref[at] = ((grad + local_grad[at]) * scale).astype(jnp.bfloat16)
         return 0
 
-    def send_gate(step, _):
+    def send_gate(step):
         device = peer_of(step, me, mem_count)
         remote(gate_send, gate_got.at[me], 5, device).start()
-        return 0
-
-    lax.fori_loop(1, mem_count, send_gate, 0)
+
+    far_first(mem_count, send_gate)
     lax.fori_loop(0, head_count // 2, memory_grad, 0)
 
     arrived = remote(gate_got.at[some], gate_got.at[some], 5, following)

time: 226 us -> 224 us (level)
  no operation moved by 1% of the time
where the time goes in v4:
time: 224 us
  Pallas kernels  223 us (100%)
    pallas_call x1, Pallas kernels, local(): pl.pallas_call(functools.partial(kernel, mem_count, head_count, pick_coun...  222 us

profile of v4, /device:TPU:6, one launch (start us, length us, event | category | flops | bytes accessed | tf_op | source)
XLA Modules:
  0.0 224.1 jit_solution(297799983690990007)
XLA Ops:
  0.6 221.6 %retrieve_attend.1 = (bf16[256,2048]{1,0:T(8,128)(2,1)S(1)}, bf16[256,2048]{1,0:T(8,128)(2,1)S(1)}, f32[1,128]{1,0:T(1,128)S(1)}) custom-call(bf16[256,2048]{1,0:T(8,128)(2,1)} %q_hbm.1, bf16[256,2048]{1,0:T(8,128)(2,1)} %g_hbm.1, bf16[6,128,2048]{2,1,0:T(8,128)(2,1)} %mk_hbm.1, bf16[6,128,2048]{2,1,0:T(8,128)(2,1)} %mv_hbm.1, bf16[2,128,2048]{2,1,0:T(8,128)(2,1)} %pk_hbm.1, ...), custom_call_target="tpu_custom_call" | custom-call | tf_op jit(solution)/shard_map/retrieve_attend/pallas_call | solution.py:422
  222.2 1.8 publish.1

commit v5 on v4

--- a/solution.py
+++ b/solution.py
@@ -160,6 +160,7 @@
     scale = dim**-0.5
     cap = 2
     peers = mem_count - 1
+    together = 4
 
     barrier = pltpu.get_barrier_semaphore()
 
@@ -191,14 +192,6 @@
 
     load_table(mk_hbm, k_table, 0, 0)
     load_table(pk_hbm, k_table, stored, 1)
-    load_table(mv_hbm, v_table, 0, 2)
-    load_table(pv_hbm, v_table, stored, 3)
-    loads = [
-        pltpu.make_async_copy(q_hbm, q_buf, load_sems.at[4]),
-        pltpu.make_async_copy(g_hbm, g_buf, load_sems.at[5]),
-    ]
-    for load in loads:
-        load.start()
     asked, where, place = route(
         top_ref, location_ref, write_ref, mem_count, head_count, stored, cap
     )
@@ -233,6 +226,14 @@
     halo_v = remote(pv_hbm.at[query_count - 1], halo.at[1], 2, following)
     halo_k.start()
     halo_v.start()
+    load_table(mv_hbm, v_table, 0, 2)
+    load_table(pv_hbm, v_table, stored, 3)
+    loads = [
+        pltpu.make_async_copy(q_hbm, q_buf, load_sems.at[4]),
+        pltpu.make_async_copy(g_hbm, g_buf, load_sems.at[5]),
+    ]
+    for load in loads:
+        load.start()
 
     some = pl.ds(0, peers)
     remote(codes_ref.at[some], code_got.at[some], 0, following).wait()
@@ -240,8 +241,6 @@
     code_copy.start()
     await_table(mk_hbm, k_table, 0)
     await_table(pk_hbm, k_table, 1)
-    await_table(mv_hbm, v_table, 2)
-    await_table(pv_hbm, v_table, 3)
     code_copy.wait()
     spots_copy.wait()
 
@@ -268,6 +267,8 @@
         send(peers)
 
     serve(k_table, k_send, k_got, 3)
+    await_table(mv_hbm, v_table, 2)
+    await_table(pv_hbm, v_table, 3)
     serve(v_table, v_send, v_got, 4)
 
     for load in loads:
@@ -335,7 +336,7 @@
     remote(v_send.at[everyone], v_got.at[everyone], 4, following).wait()
 
     def memory_result(step, _):
-        for h in (step * 2, step * 2 + 1):
+        for h in [step * together + i for i in range(together)]:
             mix = mix_of(h)
             part = gate_part[h]
             for b in range(query_count):
@@ -348,7 +349,7 @@
             gate_part[h] = part
         return 0
 
-    lax.fori_loop(0, head_count // 2, memory_result, 0)
+    lax.fori_loop(0, head_count // together, memory_result, 0)
 
     lane_ids = lax.broadcasted_iota(jnp.int32, (1, dim), 1)
     total = jnp.zeros((1, dim), jnp.float32)
@@ -360,7 +361,7 @@
     gate_got[me] = total
 
     def memory_grad(step, _):
-        for h in (step * 2, step * 2 + 1):
+        for h in [step * together + i for i in range(together)]:
             less = 1.0 + jnp.exp(-jnp.full((1, 1), gate_ref[h], jnp.float32))
             for b in range(query_count):
                 at = places(b, h)
@@ -377,7 +378,7 @@
         remote(gate_send, gate_got.at[me], 5, device).start()
 
     far_first(mem_count, send_gate)
-    lax.fori_loop(0, head_count // 2, memory_grad, 0)
+    lax.fori_loop(0, head_count // together, memory_grad, 0)
 
     arrived = remote(gate_got.at[some], gate_got.at[some], 5, following)
     arrived.wait()

time: 224 us -> 223 us (level)
  no operation moved by 1% of the time
where the time goes in v5:
time: 223 us
  Pallas kernels  222 us (100%)
    pallas_call x1, Pallas kernels, local(): pl.pallas_call(functools.partial(kernel, mem_count, head_count, pick_coun...  220 us

profile of v5, /device:TPU:6, one launch (start us, length us, event | category | flops | bytes accessed | tf_op | source)
XLA Modules:
  0.0 222.6 jit_solution(6273841413484392119)
XLA Ops:
  0.6 220.1 %retrieve_attend.1 = (bf16[256,2048]{1,0:T(8,128)(2,1)S(1)}, bf16[256,2048]{1,0:T(8,128)(2,1)S(1)}, f32[1,128]{1,0:T(1,128)S(1)}) custom-call(bf16[256,2048]{1,0:T(8,128)(2,1)} %q_hbm.1, bf16[256,2048]{1,0:T(8,128)(2,1)} %g_hbm.1, bf16[6,128,2048]{2,1,0:T(8,128)(2,1)} %mk_hbm.1, bf16[6,128,2048]{2,1,0:T(8,128)(2,1)} %mv_hbm.1, bf16[2,128,2048]{2,1,0:T(8,128)(2,1)} %pk_hbm.1, ...), custom_call_target="tpu_custom_call" | custom-call | tf_op jit(solution)/shard_map/retrieve_attend/pallas_call | solution.py:423
  220.8 1.8 publish.1

commit v6 on v5

--- a/solution.py
+++ b/solution.py
@@ -190,8 +190,6 @@
         whole = table.at[pl.ds(0, head_count * source.shape[0])]
         pltpu.make_async_copy(whole, whole, load_sems.at[which]).wait()
 
-    load_table(mk_hbm, k_table, 0, 0)
-    load_table(pk_hbm, k_table, stored, 1)
     asked, where, place = route(
         top_ref, location_ref, write_ref, mem_count, head_count, stored, cap
     )
@@ -226,6 +224,8 @@
     halo_v = remote(pv_hbm.at[query_count - 1], halo.at[1], 2, following)
     halo_k.start()
     halo_v.start()
+    load_table(mk_hbm, k_table, 0, 0)
+    load_table(pk_hbm, k_table, stored, 1)
     load_table(mv_hbm, v_table, 0, 2)
     load_table(pv_hbm, v_table, stored, 3)
     loads = [
@@ -386,10 +386,13 @@
 
 
 def publish(att_ref, qg_ref, gate_ref, att_hbm, qg_hbm, gate_out, sems):
-    copies = [
-        pltpu.make_async_copy(att_ref, att_hbm, sems.at[0]),
-        pltpu.make_async_copy(qg_ref, qg_hbm, sems.at[1]),
-    ]
+    parts = sems.shape[1]
+    size = att_ref.shape[0] // parts
+    copies = []
+    for i in range(parts):
+        rows = pl.ds(i * size, size)
+        for which, (ref, hbm) in enumerate(((att_ref, att_hbm), (qg_ref, qg_hbm))):
+            copies.append(pltpu.make_async_copy(ref.at[rows], hbm.at[rows], sems.at[which, i]))
     for copy in copies:
         copy.start()
     gate_out[...] = gate_ref[0, : gate_out.shape[0]]
@@ -480,7 +483,7 @@
         ),
         in_specs=[vmem] * 3,
         out_specs=(any_space, any_space, vmem),
-        scratch_shapes=[pltpu.SemaphoreType.DMA((2,))],
+        scratch_shapes=[pltpu.SemaphoreType.DMA((2, 4))],
         name="publish",
     )(*(pltpu.with_memory_space_constraint(x, pltpu.VMEM) for x in (attended, query_grad, gate)))
 

time: 223 us -> 223 us (level)
  no operation moved by 1% of the time
where the time goes in v6:
time: 223 us
  Pallas kernels  222 us (100%)
    pallas_call x1, Pallas kernels, local(): pl.pallas_call(functools.partial(kernel, mem_count, head_count, pick_coun...  220 us

profile of v6, /device:TPU:6, one launch (start us, length us, event | category | flops | bytes accessed | tf_op | source)
XLA Modules:
  0.0 222.6 jit_solution(8121222657785490036)
XLA Ops:
  0.6 220.1 %retrieve_attend.1 = (bf16[256,2048]{1,0:T(8,128)(2,1)S(1)}, bf16[256,2048]{1,0:T(8,128)(2,1)S(1)}, f32[1,128]{1,0:T(1,128)S(1)}) custom-call(bf16[256,2048]{1,0:T(8,128)(2,1)} %q_hbm.1, bf16[256,2048]{1,0:T(8,128)(2,1)} %g_hbm.1, bf16[6,128,2048]{2,1,0:T(8,128)(2,1)} %mk_hbm.1, bf16[6,128,2048]{2,1,0:T(8,128)(2,1)} %mv_hbm.1, bf16[2,128,2048]{2,1,0:T(8,128)(2,1)} %pk_hbm.1, ...), custom_call_target="tpu_custom_call" | custom-call | tf_op jit(solution)/shard_map/retrieve_attend/pallas_call | solution.py:426
  220.7 1.9 publish.1

commit v7 on v6

--- a/solution.py
+++ b/solution.py
@@ -161,6 +161,7 @@
     cap = 2
     peers = mem_count - 1
     together = 4
+    result_heads = 8
 
     barrier = pltpu.get_barrier_semaphore()
 
@@ -336,7 +337,7 @@
     remote(v_send.at[everyone], v_got.at[everyone], 4, following).wait()
 
     def memory_result(step, _):
-        for h in [step * together + i for i in range(together)]:
+        for h in [step * result_heads + i for i in range(result_heads)]:
             mix = mix_of(h)
             part = gate_part[h]
             for b in range(query_count):
@@ -349,7 +350,7 @@
             gate_part[h] = part
         return 0
 
-    lax.fori_loop(0, head_count // together, memory_result, 0)
+    lax.fori_loop(0, head_count // result_heads, memory_result, 0)
 
     lane_ids = lax.broadcasted_iota(jnp.int32, (1, dim), 1)
     total = jnp.zeros((1, dim), jnp.float32)

time: 223 us -> 222 us (level)
  no operation moved by 1% of the time
where the time goes in v7:
time: 222 us
  Pallas kernels  222 us (100%)
    pallas_call x1, Pallas kernels, local(): pl.pallas_call(functools.partial(kernel, mem_count, head_count, pick_coun...  220 us

profile of v7, /device:TPU:6, one launch (start us, length us, event | category | flops | bytes accessed | tf_op | source)
XLA Modules:
  0.0 222.3 jit_solution(3535946812701575007)
XLA Ops:
  0.6 219.8 %retrieve_attend.1 = (bf16[256,2048]{1,0:T(8,128)(2,1)S(1)}, bf16[256,2048]{1,0:T(8,128)(2,1)S(1)}, f32[1,128]{1,0:T(1,128)S(1)}) custom-call(bf16[256,2048]{1,0:T(8,128)(2,1)} %q_hbm.1, bf16[256,2048]{1,0:T(8,128)(2,1)} %g_hbm.1, bf16[6,128,2048]{2,1,0:T(8,128)(2,1)} %mk_hbm.1, bf16[6,128,2048]{2,1,0:T(8,128)(2,1)} %mv_hbm.1, bf16[2,128,2048]{2,1,0:T(8,128)(2,1)} %pk_hbm.1, ...), custom_call_target="tpu_custom_call" | custom-call | tf_op jit(solution)/shard_map/retrieve_attend/pallas_call | solution.py:427
  220.4 1.9 publish.1
